TPU v7x, 128 devices: a whole 4x4x4 slice. The times are simulated.
128 devices in a mesh: dp: 32 (over z, x, core), rep: 4 (over y).
Axes of the slice: x: 4, y: 4, z: 4, core: 2. Of those that a mesh axis runs over, the one named last changes fastest.
Arguments:
- token_inputs: bfloat16 [65536, 2048], P(('dp', 'rep')), may hold values from -12 to 12
- cotangent: bfloat16 [65536, 2048], P(('dp', 'rep')), may hold values from -24 to 24
- gate_preact: bfloat16 [65536, 768], P(('dp', 'rep')), may hold values from -6 to 6
- up_preact: bfloat16 [65536, 768], P(('dp', 'rep')), may hold values from -6 to 6
- down_weight: bfloat16 [2, 768, 2048], P(None, None, 'dp'), may hold values from -0.21875 to 0.21875
- block_expert: int32 [512], P(('dp', 'rep')), may hold values from 0 to 1
- block_count: int32 [512], P(('dp', 'rep')), may hold values from 1 to 128, as said below
Outputs:
- update: bfloat16 [2, 3, 768, 2048], P(None, None, None, 'dp')
Inputs may be any that keep to these rules, and one draw needn't show every extreme that they name: `block_count`: live rows of a block, at most 128; in every draw some block is full.
All inputs are finite; a program needn't handle non-finite values.
Results may differ from a plain program's by a relative error of at most 0.02.
Values may be sent and summed in bfloat16 or wider, within the bound.
No kernel may reach another device: no remote copies, remote signals or barrier semaphores. Data moves between devices by JAX's collectives and lax.ppermute only.
A program may use at most 128 MiB of HBM per device.

v0:
```python
import math
import jax
import jax.numpy as jnp
from jax import lax
from jax.sharding import Mesh
from jax.sharding import PartitionSpec as P

D = 2048
ITERS = 2
DP = ("dp_0", "dp_1", "dp_2")
DP_REP = ("dp_0", "dp_1", "dp_2", "rep")
ns_first = 3.4445
ns_second = -4.775
ns_third = 2.0315
norm_eps = 1e-07


def cut_along(value, dim, count):
    shape = value.shape
    blocks = value.reshape(*shape[:dim], count, shape[dim] // count, *shape[dim + 1 :])
    return jnp.moveaxis(blocks, dim, 0)


def sum_by_chip(value, chips, core, dim):
    sizes = (lax.axis_size(chips), lax.axis_size(core))
    blocks = cut_along(value, dim, sizes[0] * sizes[1])
    inside = blocks.shape[1:]
    blocks = blocks.reshape(*sizes, *inside).swapaxes(0, 1).reshape(-1, *inside)
    blocks = lax.psum_scatter(blocks, core, scatter_dimension=0, tiled=True)
    return lax.psum_scatter(blocks, chips, scatter_dimension=0, tiled=True)[0]


def copy_for_each(value, axis):
    count = lax.axis_size(axis)
    return lax.all_to_all(
        jnp.broadcast_to(value[None], (count, *value.shape)), axis, 0, 0, tiled=True
    )


def of_everyone(value, axis):
    everything = copy_for_each(value, axis)
    return jnp.sum(everything.astype(jnp.float32), axis=0)


def taken_together(value, axis):
    everything = copy_for_each(value, axis)
    return jnp.sum(everything, axis=0)


def whole_sweeps(matrix, column_width, groups_all, sweeps, scale):
    hidden_width = matrix.shape[0]
    group = math.gcd(8, groups_all)
    current = matrix
    result = None
    for sweep in range(sweeps):

        def add_group(index, total):
            cols = lax.dynamic_slice_in_dim(
                current, index * group * column_width, group * column_width, 1
            )
            cols = cols.reshape(hidden_width, group, column_width)
            term = jnp.einsum(
                "fnd,gnd->nfg", cols, cols, preferred_element_type=jnp.float32
            ).astype(jnp.bfloat16)
            return total + jnp.sum(lax.optimization_barrier(term).astype(jnp.float32), axis=0)

        gram = lax.fori_loop(
            0, groups_all // group, add_group, jnp.zeros((hidden_width, hidden_width), jnp.float32)
        )
        gram_half = gram.astype(jnp.bfloat16)
        squared = jnp.dot(gram_half, gram_half, preferred_element_type=jnp.float32)
        poly = (ns_second * gram + ns_third * squared).astype(jnp.bfloat16)
        newer = ns_first * current.astype(jnp.float32) + jnp.dot(
            poly, current, preferred_element_type=jnp.float32
        )
        if sweep + 1 < sweeps:
            current = newer.astype(jnp.bfloat16)
        else:
            result = (scale * newer).astype(jnp.bfloat16)
    return result


def per_device(
    token_inputs, cotangent, gate_preact, up_preact, down_weight, block_expert, block_count
):
    blocks = block_count.shape[0]
    rows_here = token_inputs.shape[0]
    hidden_width = gate_preact.shape[1]
    width = token_inputs.shape[1]
    block_rows = rows_here // blocks
    experts_here = down_weight.shape[0]
    row_place = jnp.arange(rows_here, dtype=jnp.int32) % block_rows
    row_count = jnp.repeat(block_count, block_rows, total_repeat_length=rows_here)
    row_expert = jnp.repeat(block_expert, block_rows, total_repeat_length=rows_here)
    live_rows = row_place < row_count
    masked = jnp.where(live_rows[:, None], cotangent, jnp.zeros_like(cotangent))
    gate = gate_preact.astype(jnp.float32)
    upper = up_preact.astype(jnp.float32)
    sigmoid_gate = jax.nn.sigmoid(gate)
    hidden = (gate * sigmoid_gate * upper).astype(jnp.bfloat16)
    selector = (row_expert[None, :] == jnp.arange(experts_here, dtype=jnp.int32)[:, None]).astype(
        jnp.bfloat16
    )
    masked_each = masked[None, :, :] * selector[:, :, None]
    weights_all = lax.all_gather(down_weight, DP, axis=2, tiled=True)
    back = jnp.einsum("erd,efd->rf", masked_each, weights_all, preferred_element_type=jnp.float32)
    grad_gate = (back * upper * sigmoid_gate * (1.0 + gate * (1.0 - sigmoid_gate))).astype(
        jnp.bfloat16
    )
    grad_up = (back * gate * sigmoid_gate).astype(jnp.bfloat16)
    gate_up = jnp.concatenate([grad_gate, grad_up], axis=1)
    gate_up_each = gate_up[None, :, :] * selector[:, :, None]
    hidden_each = hidden[None, :, :] * selector[:, :, None]
    input_part = jnp.einsum(
        "erf,rd->efd", gate_up_each, token_inputs, preferred_element_type=jnp.float32
    )
    output_part = jnp.einsum("erf,rd->efd", hidden_each, masked, preferred_element_type=jnp.float32)
    partial_value = jnp.concatenate(
        [input_part.reshape(experts_here, 2, hidden_width, width), output_part[:, None]], axis=1
    )
    partial_half = partial_value.astype(jnp.bfloat16)
    terms = lax.optimization_barrier(partial_half).astype(jnp.float32)
    grad = sum_by_chip(terms.astype(jnp.bfloat16), ("dp_0", "dp_1"), "dp_2", 3).astype(jnp.float32)
    grad = of_everyone(grad.astype(jnp.bfloat16), "rep").astype(jnp.float32)
    squares = taken_together(jnp.sum(grad * grad, axis=(2, 3)), DP)
    current = (grad / (jnp.sqrt(squares) + norm_eps)[:, :, None, None]).astype(jnp.bfloat16)
    column_width = current.shape[3]
    scale = jnp.sqrt(jnp.float32(D))
    result = None
    n_dp = lax.axis_size(DP)
    matrices = experts_here * 3
    flat = current.reshape(matrices, hidden_width, column_width)
    padding = jnp.zeros((n_dp - matrices, hidden_width, column_width), jnp.bfloat16)
    outbound = jnp.concatenate([flat, padding], axis=0)
    owned = lax.all_to_all(outbound, DP, split_axis=0, concat_axis=2, tiled=True)
    finished = whole_sweeps(owned[0], column_width, n_dp, ITERS, scale)
    returned = lax.all_to_all(finished[None], DP, split_axis=2, concat_axis=0, tiled=True)
    result = returned[:matrices].reshape(experts_here, 3, hidden_width, column_width)
    return result


def solution(mesh):
    torus = Mesh(mesh.devices.reshape(4, 4, 2, mesh.shape["rep"]), ("dp_0", "dp_1", "dp_2", "rep"))
    return jax.shard_map(
        per_device,
        mesh=torus,
        in_specs=(
            P(DP_REP, None),
            P(DP_REP, None),
            P(DP_REP, None),
            P(DP_REP, None),
            P(None, None, DP),
            P(DP_REP),
            P(DP_REP),
        ),
        out_specs=P(None, None, None, DP),
        check_vma=False,
    )
```

profile of v0, /device:TPU:1, one launch (start us, length us, event | category | flops | bytes accessed | tf_op | source)
XLA Modules:
  0.0 566.8 jit_solution(1773095210929279019)
XLA Ops:
  7.3 1.4 fusion.42
  8.7 2.5 fusion.30
  11.2 1.4 fusion.41
  12.6 2.5 select_select_fusion
  15.2 3.2 broadcast_select_fusion
  18.3 44.0 %all-gather.2.cloned.1.call-done = bf16[2,768,2048]{1,2,0:T(8,128)(2,1)} async-done(((bf16[2,768,64]{1,2,0:T(8,128)(2,1)}), bf16[2,768,2048]{1,2,0:T(8,128)(2,1)}) %all-gather.2.cloned.1.call-update) | async-done | bytes 6291472 | tf_op jit(solution)/shard_map/all_gather | solution.py:105
  62.4 7.8 %fusion.10 = (bf16[512,768]{1,0:T(8,128)(2,1)S(1)}, bf16[512,768]{1,0:T(8,128)(2,1)S(1)}, bf16[512,768]{1,0:T(8,128)(2,1)S(1)}) fusion(bf16[512,768]{1,0:T(8,128)(2,1)} %param.20, bf16[512,768]{1,0:T(8,128)(2,1)} %param.19, bf16[2,768,2048]{1,2,0:T(8,128)(2,1)} %all-gather.2.cloned.1.call-done, bf16[2,512]{1,0:T(2,128)(2,1)S(1)} %compare_convert_fusion, ...), kind=kOutput, calls=%fused_computation.33 | convolution fusion | flops 3230400512 | bytes 12322816 | tf_op jit(solution)/shard_map/erd,efd->rf/dot_general | solution.py:106
  71.4 2.6 copy.51
  74.0 10.6 %convolution_convert_fusion.2 = bf16[2,1536,2048]{2,1,0:T(8,128)(2,1)} fusion(bf16[512,2048]{1,0:T(8,128)(2,1)S(1)} %copy-done, bf16[2,512]{1,0:T(2,128)(2,1)S(1)} %compare_convert_fusion, bf16[512,1536]{0,1:T(8,128)(2,1)} %copy.51), kind=kOutput, calls=%fused_computation.9 | convolution fusion | flops 6450315264 | bytes 16254976 | tf_op jit(solution)/shard_map/erf,rd->efd/dot_general | solution.py:114
  84.7 16.8 %copy.53 = bf16[2,2,768,2048]{2,3,1,0:T(8,128)(2,1)} copy(bf16[2,2,768,2048]{3,2,1,0:T(8,128)(2,1)} %bitcast.100) | data formatting | bytes 25165824 | tf_op jit(solution)/shard_map/reshape | solution.py:119
  102.6 6.3 %convert_bitcast_fusion = bf16[2,1,768,2048]{3,2,0,1:T(8,128)(2,1)} fusion(bf16[512,2048]{1,0:T(8,128)(2,1)S(1)} %copy-done.2, bf16[2,512]{1,0:T(2,128)(2,1)S(1)} %compare_convert_fusion, bf16[512,768]{0,1:T(8,128)(2,1)} %copy.52), kind=kOutput, calls=%fused_computation.12 | convolution fusion | flops 3225157632 | bytes 9177088 | tf_op jit(solution)/shard_map/erf,rd->efd/dot_general | solution.py:117
  108.9 8.7 %copy.54 = bf16[2,1,768,2048]{2,3,1,0:T(8,128)(2,1)} copy(bf16[2,1,768,2048]{3,2,0,1:T(8,128)(2,1)} %convert_bitcast_fusion) | data formatting | bytes 12582912 | tf_op jit(solution)/shard_map/broadcast_in_dim | solution.py:119
  117.6 9.5 %pad_maximum_fusion = bf16[2,3,768,2048]{2,3,1,0:T(8,128)(2,1)S(1)} fusion(bf16[2,1,768,2048]{2,3,1,0:T(8,128)(2,1)} %copy.54, bf16[2,2,768,2048]{2,3,1,0:T(8,128)(2,1)} %copy.53), kind=kLoop, calls=%fused_computation.8 | loop fusion | flops 9437184 | bytes 37748736 | tf_op jit(solution)/shard_map/concatenate | solution.py:118
  127.1 6.7 %copy.55 = bf16[16,2,2,3,768,64]{4,5,3,2,0,1:T(8,128)(2,1)} copy(bf16[16,2,2,3,768,64]{4,5,1,0,3,2:T(8,128)(2,1)S(1)} %bitcast.97) | data formatting | bytes 37748736 | tf_op jit(solution)/shard_map/reshape | solution.py:28
  133.9 28.0 %reduce-scatter.5.cloned.1.call-done = bf16[16,2,3,768,64]{3,4,2,1,0:T(8,128)(2,1)} async-done(((bf16[32,2,3,768,64]{3,4,2,1,0:T(8,128)(2,1)}), bf16[16,2,3,768,64]{3,4,2,1,0:T(8,128)(2,1)}) %reduce-scatter.5.cloned.1.call-update) | async-done | bytes 9437200 | tf_op jit(solution)/shard_map/reduce_scatter | solution.py:29
  161.9 91.3 %reduce-scatter.7.cloned.1.call-done = bf16[1,2,3,768,64]{3,4,2,1,0:T(8,128)(2,1)} async-done(((bf16[16,2,3,768,64]{3,4,2,1,0:T(8,128)(2,1)}), bf16[1,2,3,768,64]{3,4,2,1,0:T(8,128)(2,1)}) %reduce-scatter.7.cloned.1.call-update) | async-done | bytes 589840
  254.5 30.7 %all_to_all.40 = bf16[4,2,3,768,64]{3,4,2,1,0:T(8,128)(2,1)S(1)} all-to-all(bf16[4,2,3,768,64]{3,4,2,1,0:T(8,128)(2,1)S(1)} %broadcast_in_dim.31), channel_id=1, replica_groups=mesh['dp_0'=4,'dp_1'=4,'dp_2'=2,'rep'=4] {'rep'}, dimensions={0} | all-to-all | bytes 4718592 | tf_op jit(solution)/shard_map/all_to_all | solution.py:35
  285.8 15.0 %all_to_all.41 = f32[32,2,3]{2,1,0:T(2,128)S(1)} all-to-all(f32[32,2,3]{2,1,0:T(2,128)S(1)} %broadcast_in_dim.32), channel_id=1, replica_groups=mesh['dp_0'=4,'dp_1'=4,'dp_2'=2,'rep'=4] {'dp_0','dp_1','dp_2'}, dimensions={0} | all-to-all | bytes 1536 | tf_op jit(solution)/shard_map/all_to_all | solution.py:35
  301.3 2.0 concatenate.18
  303.3 5.0 all-to-all-start.2
  308.3 39.9 %all-to-all-done.2 = bf16[32,768,64]{1,2,0:T(8,128)(2,1)} async-done(((bf16[32,768,64]{1,2,0:T(8,128)(2,1)}), bf16[32,768,64]{1,2,0:T(8,128)(2,1)}, u32[]{:S(2)}, u32[]{:S(2)}) %all-to-all-start.2) | async-done | bytes 3145760 | tf_op jit(solution)/shard_map/all_to_all | solution.py:135
  348.2 4.7 copy.58
  352.9 33.6 %while.34 = (s32[]{:T(128)}, f32[768,768]{1,0:T(8,128)}, bf16[768,2048]{0,1:T(8,128)(2,1)}, s32[]{:T(128)}, s32[]{:T(128)}, /*index=5*/s32[]{:T(128)}, s32[]{:T(128)}) while((s32[]{:T(128)}, f32[768,768]{1,0:T(8,128)}, bf16[768,2048]{0,1:T(8,128)(2,1)}, s32[]{:T(128)}, s32[]{:T(128)}, /*index=5*/s32[]{:T(128)}, s32[]{:T(128)}) %tuple.98), condition=%wide.region_7.9_spmd.clone, body=%wide.region_5.8_spmd.clone.sunk | while | flops 618725376 | bytes 30670984 | solution.py:67
  354.1 2.9 convolution_convert_fusion.5
  358.3 1.8 select_add_fusion.4
  361.3 2.9 convolution_convert_fusion.5
  365.4 3.4 select_add_fusion.4
  370.1 2.9 convolution_convert_fusion.5
  374.2 3.4 select_add_fusion.4
  378.9 2.9 convolution_convert_fusion.5
  383.0 3.4 select_add_fusion.4
  386.5 10.5 %add_convert_fusion = bf16[768,2048]{1,0:T(8,128)(2,1)} fusion(bf16[768,2048]{1,0:T(8,128)(2,1)} %copy.58, bf16[768,2048]{0,1:T(8,128)(2,1)} %bitcast.23, f32[768,768]{1,0:T(8,128)} %get-tuple-element.202), kind=kOutput, calls=%fused_computation.11 | convolution fusion | flops 3331129344 | bytes 11796480 | tf_op jit(solution)/shard_map/dot_general | solution.py:73
  397.0 34.4 %while.35 = (s32[]{:T(128)}, f32[768,768]{1,0:T(8,128)}, bf16[768,2048]{1,0:T(8,128)(2,1)}, s32[]{:T(128)}, s32[]{:T(128)}, /*index=5*/s32[]{:T(128)}, s32[]{:T(128)}) while((s32[]{:T(128)}, f32[768,768]{1,0:T(8,128)}, bf16[768,2048]{1,0:T(8,128)(2,1)}, s32[]{:T(128)}, s32[]{:T(128)}, /*index=5*/s32[]{:T(128)}, s32[]{:T(128)}) %tuple.101), condition=%wide.region_10.12_spmd.clone, body=%wide.region_8.11_spmd.clone.sunk | while | flops 618725376 | bytes 32243848 | solution.py:67
  398.4 2.9 convolution_convert_fusion.6
  402.6 1.7 select_add_fusion.5
  405.8 2.9 convolution_convert_fusion.6
  410.0 3.4 select_add_fusion.5
  414.8 2.9 convolution_convert_fusion.6
  419.0 3.4 select_add_fusion.5
  423.8 2.9 convolution_convert_fusion.6
  428.0 3.4 select_add_fusion.5
  431.4 8.5 %fusion.3 = bf16[1,768,2048]{2,1,0:T(8,128)(2,1)S(1)} fusion(bf16[768,2048]{1,0:T(8,128)(2,1)} %get-tuple-element.360, f32[768,768]{1,0:T(8,128)} %get-tuple-element.203), kind=kOutput, calls=%fused_computation.17 | convolution fusion | flops 3332702208 | bytes 8650752 | tf_op jit(solution)/shard_map/dot_general | solution.py:73
  439.9 11.2 %copy.60 = bf16[1,768,2048]{1,0,2:T(2,128)(2,1)} copy(bf16[1,768,2048]{2,1,0:T(8,128)(2,1)S(1)} %fusion.3) | data formatting | bytes 6291456 | tf_op jit(solution)/shard_map/broadcast_in_dim | solution.py:137
  451.7 33.3 %reduce.3 = bf16[2048,768]{1,0:T(8,128)(2,1)} reduce(bf16[2048,1,768]{2,1,0:T(2,128)(2,1)} %bitcast.98, bf16[]{:T(256)} %broadcast.220), dimensions={1}, to_apply=%bitcast.73.reduce_sub_computation | reduce | bytes 6291458
  485.0 6.6 %reshape.174 = bf16[32,2,24576]{2,1,0:T(2,128)(2,1)S(1)} reshape(bf16[2048,768]{1,0:T(8,128)(2,1)} %reduce.3) | data formatting | bytes 6291456
  491.6 45.5 %all_to_all.42 = bf16[32,2,24576]{2,1,0:T(2,128)(2,1)} all-to-all(bf16[32,2,24576]{2,1,0:T(2,128)(2,1)S(1)} %reshape.174), channel_id=1, replica_groups=mesh['dp_0'=4,'dp_1'=4,'dp_2'=2,'rep'=4] {'dp_0','dp_1','dp_2'}, dimensions={0} | all-to-all | bytes 6291456 | tf_op jit(solution)/shard_map/all_to_all | solution.py:137
  537.1 18.9 %reshape.175 = bf16[2048,1,768]{2,1,0:T(2,128)(2,1)} reshape(bf16[32,2,24576]{2,1,0:T(2,128)(2,1)} %all_to_all.42) | data formatting | bytes 6291456
  556.0 3.5 copy.62
  (49 shorter events, 27.6 us)
Async XLA Ops:
  6.5 67.5 %copy-start = (bf16[512,2048]{1,0:T(8,128)(2,1)S(1)}, bf16[512,2048]{1,0:T(8,128)(2,1)}, u32[]{:S(2)}) copy-start(bf16[512,2048]{1,0:T(8,128)(2,1)} %param.17) | copy-start | bytes 6291460
  6.5 55.8 %all-gather.2.cloned.1.call-start = ((), (), s32[]{:S(2)}) async-start(), calls=%async_computation.6 | async-start | bytes 6488064 | tf_op jit(solution)/shard_map/all_gather | solution.py:105
  7.3 154.6 %reduce-scatter.5.cloned.1.call-start = ((), (), s32[]{:S(2)}) async-start(), calls=%async_computation.7 | async-start | bytes 28311552 | tf_op jit(solution)/shard_map/reduce_scatter | solution.py:29
  84.7 18.0 %copy-start.2 = (bf16[512,2048]{1,0:T(8,128)(2,1)S(1)}, bf16[512,2048]{1,0:T(8,128)(2,1)}, u32[]{:S(2)}) copy-start(bf16[512,2048]{1,0:T(8,128)(2,1)} %broadcast_select_fusion) | copy-start | bytes 6291460
  133.8 119.4 %reduce-scatter.7.cloned.1.call-start = ((), (), s32[]{:S(2)}) async-start(), calls=%async_computation.8 | async-start | bytes 10027008
  303.3 44.9 %all-to-all-start.2 = ((bf16[32,768,64]{1,2,0:T(8,128)(2,1)}), bf16[32,768,64]{1,2,0:T(8,128)(2,1)}, u32[]{:S(2)}, u32[]{:S(2)}) async-start(bf16[32,768,64]{1,2,0:T(8,128)(2,1)} %concatenate.18), calls=%async_computation.3 | async-start | bytes 6291456 | tf_op jit(solution)/shard_map/all_to_all | solution.py:135
  556.0 4.3 copy-start.1
Sparse Core Ops, SparseCore 0:
  9.6 52.6 all-gather.1
  133.9 27.9 reduce-scatter.4
  165.4 87.7 reduce-scatter.6
where the time goes:
time: 570 us; the launch traced here: 567 us
  waiting for transfers between devices  204 us (36%)
  local copies, waits for them, and re-layouts  99.3 us (17%)
  blocking collectives  91.1 us (16%)
  other arithmetic  87 us (15%)
  matrix products  66.9 us (12%)
  between operations  13.2 us (2%)
    unnamed x4, waiting for transfers between devices  92 us
    all_to_all x2, blocking collectives, copy_for_each(): lax.all_to_all(jnp.broadcast_to(value[None], (count, *value.shape)), axis...  45.6 us
    all_to_all x1, blocking collectives, per_device(): lax.all_to_all(finished[None], DP, split_axis=2, concat_axis=0, tiled=True)  45.5 us
    all_gather x1, waiting for transfers between devices, per_device(): weights_all = lax.all_gather(down_weight, DP, axis=2, tiled=True)  44 us
    all_to_all x1, waiting for transfers between devices, per_device(): lax.all_to_all(outbound, DP, split_axis=0, concat_axis=2, tiled=True)  39.9 us
    unnamed x3, other arithmetic  33.3 us
    unnamed x11, local copies, waits for them, and re-layouts  29.6 us
    reduce_scatter x1, waiting for transfers between devices, sum_by_chip(): blocks = lax.psum_scatter(blocks, core, scatter_dimension=0, tiled=True)  28 us
  transfers between devices with their start and end apart: 4, of which 4 were waited for; matrix products, arithmetic and copies ran while one was open for 2% of the time, Pallas kernels for 0%

commit v1 on v0

--- a/solution.py
+++ b/solution.py
@@ -102,7 +102,10 @@
         jnp.bfloat16
     )
     masked_each = masked[None, :, :] * selector[:, :, None]
-    weights_all = lax.all_gather(down_weight, DP, axis=2, tiled=True)
+    size = lax.axis_size(DP)
+    pieces = jnp.stack([down_weight for _ in range(size)])
+    pieces = lax.all_to_all(pieces, DP, split_axis=0, concat_axis=0)
+    weights_all = jnp.concatenate(pieces, axis=2)
     back = jnp.einsum("erd,efd->rf", masked_each, weights_all, preferred_element_type=jnp.float32)
     grad_gate = (back * upper * sigmoid_gate * (1.0 + gate * (1.0 - sigmoid_gate))).astype(
         jnp.bfloat16

time: 570 us -> 605 us (1.061)
  waiting for transfers between devices: 204 us -> 226 us
  starting transfers between devices: 5.05 us -> 14.5 us
  local copies, waits for them, and re-layouts: 99.3 us -> 106 us
    all_to_all x0 -> x1, waiting for transfers between devices: none -> 63.9 us  [per_device(): pieces = lax.all_to_all(pieces, DP, split_axis=0, concat_axis=0)]
    all_gather x1 -> x0, waiting for transfers between devices: 44 us -> none  [per_device(): weights_all = lax.all_gather(down_weight, DP, axis=2, tiled=True)]
    all_to_all x0 -> x1, starting transfers between devices: none -> 9.6 us  [per_device(): pieces = lax.all_to_all(pieces, DP, split_axis=0, concat_axis=0)]
    unnamed x4 -> x3, waiting for transfers between devices: 92 us -> 91.4 us
    unnamed x11 -> x21, local copies, waits for them, and re-layouts: 29.6 us -> 30 us
where the time goes in v1:
time: 605 us; the launch traced here: 602 us
  waiting for transfers between devices  226 us (37%)
  local copies, waits for them, and re-layouts  106 us (18%)
  blocking collectives  91.5 us (15%)
  other arithmetic  87.1 us (14%)
  matrix products  63.2 us (10%)
  starting transfers between devices  14.5 us (2%)
  between operations  13.6 us (2%)
    unnamed x3, waiting for transfers between devices  91.4 us
    all_to_all x1, waiting for transfers between devices, per_device(): pieces = lax.all_to_all(pieces, DP, split_axis=0, concat_axis=0)  63.9 us
    all_to_all x1, blocking collectives, per_device(): lax.all_to_all(finished[None], DP, split_axis=2, concat_axis=0, tiled=True)  45.8 us
    all_to_all x2, blocking collectives, copy_for_each(): lax.all_to_all(jnp.broadcast_to(value[None], (count, *value.shape)), axis...  45.7 us
    all_to_all x1, waiting for transfers between devices, per_device(): lax.all_to_all(outbound, DP, split_axis=0, concat_axis=2, tiled=True)  39.5 us
    unnamed x3, other arithmetic  33.3 us
    reduce_scatter x1, waiting for transfers between devices, sum_by_chip(): blocks = lax.psum_scatter(blocks, core, scatter_dimension=0, tiled=True)  30.7 us
    unnamed x21, local copies, waits for them, and re-layouts  30 us
  transfers between devices with their start and end apart: 4, of which 4 were waited for; matrix products, arithmetic and copies ran while one was open for 2% of the time, Pallas kernels for 0%

profile of v1, /device:TPU:1, one launch (start us, length us, event | category | flops | bytes accessed | tf_op | source)
XLA Modules:
  0.0 601.8 jit_solution(14223609903028535106)
XLA Ops:
  6.5 4.5 stack.2
  11.0 9.6 %all-to-all-start = ((bf16[32,2,768,64]{2,3,1,0:T(8,128)(2,1)}), bf16[32,2,768,64]{2,3,1,0:T(8,128)(2,1)}, u32[]{:S(2)}, u32[]{:S(2)}) async-start(bf16[32,2,768,64]{2,3,1,0:T(8,128)(2,1)} %stack.2), calls=%async_computation | async-start | bytes 12582912 | tf_op jit(solution)/shard_map/all_to_all | solution.py:107
  21.4 2.6 fusion.30
  24.6 2.6 select_select_fusion
  27.2 3.2 broadcast_select_fusion
  30.4 63.9 %all-to-all-done = bf16[32,2,768,64]{2,3,1,0:T(8,128)(2,1)} async-done(((bf16[32,2,768,64]{2,3,1,0:T(8,128)(2,1)}), bf16[32,2,768,64]{2,3,1,0:T(8,128)(2,1)}, u32[]{:S(2)}, u32[]{:S(2)}) %all-to-all-start) | async-done | bytes 6291488 | tf_op jit(solution)/shard_map/all_to_all | solution.py:107
  94.3 3.3 copy.59
  98.1 4.1 fusion.10
  103.4 2.6 copy.61
  106.1 10.6 %convolution_convert_fusion.2 = bf16[2,1536,2048]{2,1,0:T(8,128)(2,1)} fusion(bf16[512,2048]{1,0:T(8,128)(2,1)S(1)} %copy-done, bf16[2,512]{1,0:T(2,128)(2,1)S(1)} %compare_convert_fusion, bf16[512,1536]{0,1:T(8,128)(2,1)} %copy.61), kind=kOutput, calls=%fused_computation.9 | convolution fusion | flops 6450315264 | bytes 16254976 | tf_op jit(solution)/shard_map/erf,rd->efd/dot_general | solution.py:117
  116.7 16.8 %copy.63 = bf16[2,2,768,2048]{2,3,1,0:T(8,128)(2,1)} copy(bf16[2,2,768,2048]{3,2,1,0:T(8,128)(2,1)} %bitcast.103) | data formatting | bytes 25165824 | tf_op jit(solution)/shard_map/reshape | solution.py:122
  134.7 6.3 %convert_bitcast_fusion = bf16[2,1,768,2048]{3,2,0,1:T(8,128)(2,1)} fusion(bf16[512,2048]{1,0:T(8,128)(2,1)S(1)} %copy-done.3, bf16[2,512]{1,0:T(2,128)(2,1)S(1)} %compare_convert_fusion, bf16[512,768]{0,1:T(8,128)(2,1)} %copy.62), kind=kOutput, calls=%fused_computation.12 | convolution fusion | flops 3225157632 | bytes 9177088 | tf_op jit(solution)/shard_map/erf,rd->efd/dot_general | solution.py:120
  140.9 8.7 %copy.64 = bf16[2,1,768,2048]{2,3,1,0:T(8,128)(2,1)} copy(bf16[2,1,768,2048]{3,2,0,1:T(8,128)(2,1)} %convert_bitcast_fusion) | data formatting | bytes 12582912 | tf_op jit(solution)/shard_map/broadcast_in_dim | solution.py:122
  149.6 9.5 %pad_maximum_fusion = bf16[2,3,768,2048]{2,3,1,0:T(8,128)(2,1)S(1)} fusion(bf16[2,1,768,2048]{2,3,1,0:T(8,128)(2,1)} %copy.64, bf16[2,2,768,2048]{2,3,1,0:T(8,128)(2,1)} %copy.63), kind=kLoop, calls=%fused_computation.8 | loop fusion | flops 9437184 | bytes 37748736 | tf_op jit(solution)/shard_map/concatenate | solution.py:121
  159.1 6.7 %copy.65 = bf16[16,2,2,3,768,64]{4,5,3,2,0,1:T(8,128)(2,1)} copy(bf16[16,2,2,3,768,64]{4,5,1,0,3,2:T(8,128)(2,1)S(1)} %bitcast.100) | data formatting | bytes 37748736 | tf_op jit(solution)/shard_map/reshape | solution.py:28
  165.9 30.7 %reduce-scatter.5.cloned.1.call-done = bf16[16,2,3,768,64]{3,4,2,1,0:T(8,128)(2,1)} async-done(((bf16[32,2,3,768,64]{3,4,2,1,0:T(8,128)(2,1)}), bf16[16,2,3,768,64]{3,4,2,1,0:T(8,128)(2,1)}) %reduce-scatter.5.cloned.1.call-update) | async-done | bytes 9437200 | tf_op jit(solution)/shard_map/reduce_scatter | solution.py:29
  196.6 91.4 %reduce-scatter.7.cloned.1.call-done = bf16[1,2,3,768,64]{3,4,2,1,0:T(8,128)(2,1)} async-done(((bf16[16,2,3,768,64]{3,4,2,1,0:T(8,128)(2,1)}), bf16[1,2,3,768,64]{3,4,2,1,0:T(8,128)(2,1)}) %reduce-scatter.7.cloned.1.call-update) | async-done | bytes 589840
  289.4 30.8 %all_to_all.45 = bf16[4,2,3,768,64]{3,4,2,1,0:T(8,128)(2,1)S(1)} all-to-all(bf16[4,2,3,768,64]{3,4,2,1,0:T(8,128)(2,1)S(1)} %broadcast_in_dim.31), channel_id=1, replica_groups=mesh['dp_0'=4,'dp_1'=4,'dp_2'=2,'rep'=4] {'rep'}, dimensions={0} | all-to-all | bytes 4718592 | tf_op jit(solution)/shard_map/all_to_all | solution.py:35
  320.8 14.9 %all_to_all.46 = f32[32,2,3]{2,1,0:T(2,128)S(1)} all-to-all(f32[32,2,3]{2,1,0:T(2,128)S(1)} %broadcast_in_dim.32), channel_id=1, replica_groups=mesh['dp_0'=4,'dp_1'=4,'dp_2'=2,'rep'=4] {'dp_0','dp_1','dp_2'}, dimensions={0} | all-to-all | bytes 1536 | tf_op jit(solution)/shard_map/all_to_all | solution.py:35
  336.2 2.0 concatenate.18
  338.2 4.8 all-to-all-start.3
  343.0 39.5 %all-to-all-done.3 = bf16[32,768,64]{1,2,0:T(8,128)(2,1)} async-done(((bf16[32,768,64]{1,2,0:T(8,128)(2,1)}), bf16[32,768,64]{1,2,0:T(8,128)(2,1)}, u32[]{:S(2)}, u32[]{:S(2)}) %all-to-all-start.3) | async-done | bytes 3145760 | tf_op jit(solution)/shard_map/all_to_all | solution.py:138
  382.5 4.7 copy.68
  387.2 33.6 %while.34 = (s32[]{:T(128)}, f32[768,768]{1,0:T(8,128)}, bf16[768,2048]{0,1:T(8,128)(2,1)}, s32[]{:T(128)}, s32[]{:T(128)}, /*index=5*/s32[]{:T(128)}, s32[]{:T(128)}) while((s32[]{:T(128)}, f32[768,768]{1,0:T(8,128)}, bf16[768,2048]{0,1:T(8,128)(2,1)}, s32[]{:T(128)}, s32[]{:T(128)}, /*index=5*/s32[]{:T(128)}, s32[]{:T(128)}) %tuple.98), condition=%wide.region_7.9_spmd.clone, body=%wide.region_5.8_spmd.clone.sunk | while | flops 618725376 | bytes 30670984 | solution.py:67
  388.4 2.9 convolution_convert_fusion.5
  392.6 1.8 select_add_fusion.4
  395.6 2.9 convolution_convert_fusion.5
  399.7 3.4 select_add_fusion.4
  404.4 2.9 convolution_convert_fusion.5
  408.5 3.4 select_add_fusion.4
  413.2 2.9 convolution_convert_fusion.5
  417.4 3.4 select_add_fusion.4
  420.8 10.5 %add_convert_fusion = bf16[768,2048]{1,0:T(8,128)(2,1)} fusion(bf16[768,2048]{1,0:T(8,128)(2,1)} %copy.68, bf16[768,2048]{0,1:T(8,128)(2,1)} %bitcast.25, f32[768,768]{1,0:T(8,128)} %get-tuple-element.202), kind=kOutput, calls=%fused_computation.11 | convolution fusion | flops 3331129344 | bytes 11796480 | tf_op jit(solution)/shard_map/dot_general | solution.py:73
  431.3 34.4 %while.35 = (s32[]{:T(128)}, f32[768,768]{1,0:T(8,128)}, bf16[768,2048]{1,0:T(8,128)(2,1)}, s32[]{:T(128)}, s32[]{:T(128)}, /*index=5*/s32[]{:T(128)}, s32[]{:T(128)}) while((s32[]{:T(128)}, f32[768,768]{1,0:T(8,128)}, bf16[768,2048]{1,0:T(8,128)(2,1)}, s32[]{:T(128)}, s32[]{:T(128)}, /*index=5*/s32[]{:T(128)}, s32[]{:T(128)}) %tuple.101), condition=%wide.region_10.12_spmd.clone, body=%wide.region_8.11_spmd.clone.sunk | while | flops 618725376 | bytes 32243848 | solution.py:67
  432.7 2.9 convolution_convert_fusion.6
  440.1 2.9 convolution_convert_fusion.6
  444.3 3.4 select_add_fusion.5
  449.1 2.9 convolution_convert_fusion.6
  453.3 3.4 select_add_fusion.5
  458.1 2.9 convolution_convert_fusion.6
  462.3 3.4 select_add_fusion.5
  465.7 8.5 %fusion.3 = bf16[1,768,2048]{2,1,0:T(8,128)(2,1)S(1)} fusion(bf16[768,2048]{1,0:T(8,128)(2,1)} %get-tuple-element.361, f32[768,768]{1,0:T(8,128)} %get-tuple-element.203), kind=kOutput, calls=%fused_computation.17 | convolution fusion | flops 3332702208 | bytes 8650752 | tf_op jit(solution)/shard_map/dot_general | solution.py:73
  474.3 11.2 %copy.70 = bf16[1,768,2048]{1,0,2:T(2,128)(2,1)} copy(bf16[1,768,2048]{2,1,0:T(8,128)(2,1)S(1)} %fusion.3) | data formatting | bytes 6291456 | tf_op jit(solution)/shard_map/broadcast_in_dim | solution.py:140
  486.0 33.3 %reduce.3 = bf16[2048,768]{1,0:T(8,128)(2,1)} reduce(bf16[2048,1,768]{2,1,0:T(2,128)(2,1)} %bitcast.101, bf16[]{:T(256)} %broadcast.222), dimensions={1}, to_apply=%bitcast.76.reduce_sub_computation | reduce | bytes 6291458
  519.3 6.6 %reshape.184 = bf16[32,2,24576]{2,1,0:T(2,128)(2,1)S(1)} reshape(bf16[2048,768]{1,0:T(8,128)(2,1)} %reduce.3) | data formatting | bytes 6291456
  525.9 45.8 %all_to_all.47 = bf16[32,2,24576]{2,1,0:T(2,128)(2,1)} all-to-all(bf16[32,2,24576]{2,1,0:T(2,128)(2,1)S(1)} %reshape.184), channel_id=1, replica_groups=mesh['dp_0'=4,'dp_1'=4,'dp_2'=2,'rep'=4] {'dp_0','dp_1','dp_2'}, dimensions={0} | all-to-all | bytes 6291456 | tf_op jit(solution)/shard_map/all_to_all | solution.py:140
  571.8 18.9 %reshape.185 = bf16[2048,1,768]{2,1,0:T(2,128)(2,1)} reshape(bf16[32,2,24576]{2,1,0:T(2,128)(2,1)} %all_to_all.47) | data formatting | bytes 6291456
  590.7 3.5 copy.73
  (60 shorter events, 30.4 us)
Async XLA Ops:
  6.5 99.5 %copy-start = (bf16[512,2048]{1,0:T(8,128)(2,1)S(1)}, bf16[512,2048]{1,0:T(8,128)(2,1)}, u32[]{:S(2)}) copy-start(bf16[512,2048]{1,0:T(8,128)(2,1)} %param.17) | copy-start | bytes 6291460
  11.0 9.7 %copy-start.4 = (s32[4]{0:T(128)S(1)}, s32[4]{0:T(128)}, u32[]{:S(2)}) copy-start(s32[4]{0:T(128)} %param.23) | copy-start | bytes 52
  11.0 12.9 %copy-start.5 = (s32[4]{0:T(128)S(1)}, s32[4]{0:T(128)}, u32[]{:S(2)}) copy-start(s32[4]{0:T(128)} %param.22) | copy-start | bytes 52
  11.0 83.2 %all-to-all-start = ((bf16[32,2,768,64]{2,3,1,0:T(8,128)(2,1)}), bf16[32,2,768,64]{2,3,1,0:T(8,128)(2,1)}, u32[]{:S(2)}, u32[]{:S(2)}) async-start(bf16[32,2,768,64]{2,3,1,0:T(8,128)(2,1)} %stack.2), calls=%async_computation | async-start | bytes 12582912 | tf_op jit(solution)/shard_map/all_to_all | solution.py:107
  20.6 176.0 %reduce-scatter.5.cloned.1.call-start = ((), (), s32[]{:S(2)}) async-start(), calls=%async_computation.7 | async-start | bytes 28311552 | tf_op jit(solution)/shard_map/reduce_scatter | solution.py:29
  94.3 3.4 copy-start.2
  94.3 3.6 copy-start.6
  94.3 3.8 copy-start.7
  116.7 18.0 %copy-start.3 = (bf16[512,2048]{1,0:T(8,128)(2,1)S(1)}, bf16[512,2048]{1,0:T(8,128)(2,1)}, u32[]{:S(2)}) copy-start(bf16[512,2048]{1,0:T(8,128)(2,1)} %broadcast_select_fusion) | copy-start | bytes 6291460
  165.8 122.2 %reduce-scatter.7.cloned.1.call-start = ((), (), s32[]{:S(2)}) async-start(), calls=%async_computation.8 | async-start | bytes 10027008
  338.2 44.3 %all-to-all-start.3 = ((bf16[32,768,64]{1,2,0:T(8,128)(2,1)}), bf16[32,768,64]{1,2,0:T(8,128)(2,1)}, u32[]{:S(2)}, u32[]{:S(2)}) async-start(bf16[32,768,64]{1,2,0:T(8,128)(2,1)} %concatenate.18), calls=%async_computation.4 | async-start | bytes 6291456 | tf_op jit(solution)/shard_map/all_to_all | solution.py:138
  590.7 4.3 copy-start.1
Sparse Core Ops, SparseCore 0:
  166.0 30.6 reduce-scatter.4
  200.1 87.8 reduce-scatter.6
